TPU v7x, 512 devices: a 4x2x32 block of a 4x8x32 slice. The times are simulated.
512 devices in a mesh: parts: 2 (over y), space: 32 (over z), tm: 4 (over x), spin: 2 (over core).
Axes of the slice: x: 4, y: 2, z: 32, core: 2. Of those that a mesh axis runs over, the one named last changes fastest.
The devices are a block of a 4x8x32 slice.
Arguments:
- backward: bfloat16 [4, 4, 4, 64, 3, 32, 128], P('parts', 'tm', None, 'spin', None, 'space'), parts along dimension 0, may hold values from -6 to 6
- forward: bfloat16 [4, 4, 4, 64, 3, 32, 128], P('parts', 'tm', None, 'spin', None, 'space'), parts along dimension 0, may hold values from -6 to 6
- gauge_links: bfloat16 [4, 3, 3, 3, 4, 32, 128], P('parts', None, None, None, 'tm', 'space'), parts along dimension 0, may hold values from -2.5 to 2.5
- momenta: int32 [3, 3], replicated, may hold values from -2 to 2
- gamma_list: int32 [16], replicated, may hold values from 0 to 15
Outputs:
- insertion: float32 [4, 3, 16, 4, 64, 64], P('parts', None, None, 'tm', 'space', 'spin'), parts along dimension 0
There are 2 independent parts, one for each index of `parts`. A program takes and returns all parts, laid end to end along the dimension named above; an argument that names none is the same for every part. Nothing has to cross between parts.
All inputs are finite; a program needn't handle non-finite values.
Results may differ from a plain program's by a relative error of at most 0.0056.
Values may be sent and summed in bfloat16 or wider, within the bound.
A program may use at most 64 MiB of HBM per device.

v0:
```python
import math

import jax
import jax.numpy as jnp
import numpy as np
from jax import lax
from jax.sharding import PartitionSpec as P

LX = 32


def as_sent(value):
    return jax.tree.map(lambda a: a.astype(jnp.bfloat16) if a.dtype == jnp.float32 else a, value)


def passed_along(value, axis, steps):
    count = lax.axis_size(axis)
    pairs = [(source, (source + steps) % count) for source in range(count)]
    return lax.ppermute(value, axis, pairs)


def laid_out(pieces, dim):
    lengths = list(pieces.shape[1:])
    lengths[dim] *= pieces.shape[0]
    return jnp.moveaxis(pieces, 0, dim).reshape(lengths)


def copy_for_each(value, axis):
    copies = jnp.broadcast_to(value, (lax.axis_size(axis), *value.shape))
    return lax.all_to_all(copies, axis, split_axis=0, concat_axis=0, tiled=True)


def gathered_copies(value, axis, dim):
    return laid_out(copy_for_each(value, axis), dim)


def split_up(value, dim, devices):
    before, after = (value.shape[:dim], value.shape[dim + 1 :])
    return jnp.moveaxis(value.reshape(*before, devices, -1, *after), dim, 0)


def summed_on_arrival(value, axis, dim):
    pieces = split_up(value, dim, lax.axis_size(axis))
    arrived = lax.all_to_all(pieces, axis, split_axis=0, concat_axis=0, tiled=True)
    return arrived.astype(jnp.float32).sum(axis=0)


def gamma_tables():
    zeros = np.zeros((4, 4))
    gx_imag = np.array([[0, 0, 0, 1], [0, 0, 1, 0], [0, -1, 0, 0], [-1, 0, 0, 0]]) * 1.0
    gy_real = np.array([[0, 0, 0, -1], [0, 0, 1, 0], [0, 1, 0, 0], [-1, 0, 0, 0]]) * 1.0
    gz_imag = np.array([[0, 0, 1, 0], [0, 0, 0, -1], [-1, 0, 0, 0], [0, 1, 0, 0]]) * 1.0
    gt_real = np.array([[0, 0, 1, 0], [0, 0, 0, 1], [1, 0, 0, 0], [0, 1, 0, 0]]) * 1.0
    singles = [(zeros, gx_imag), (gy_real, zeros), (zeros, gz_imag), (gt_real, zeros)]
    clif_real = []
    clif_imag = []
    for number in range(16):
        mat_real = np.eye(4)
        mat_imag = np.zeros((4, 4))
        for which in range(4):
            if number >> which & 1:
                other_real, other_imag = singles[which]
                new_real = mat_real @ other_real - mat_imag @ other_imag
                new_imag = mat_real @ other_imag + mat_imag @ other_real
                mat_real, mat_imag = (new_real, new_imag)
        clif_real.append(mat_real)
        clif_imag.append(mat_imag)
    return (singles, (np.stack(clif_real), np.stack(clif_imag)))


def chosen_gammas(gamma_list):
    singles, clifford = gamma_tables()
    table_real = jnp.asarray(clifford[0], dtype=jnp.float32)
    table_imag = jnp.asarray(clifford[1], dtype=jnp.float32)
    one_hot = (gamma_list[:, None] == jnp.arange(16, dtype=jnp.int32)[None, :]).astype(jnp.float32)
    gam_real = jnp.einsum("kg,gsv->ksv", one_hot, table_real, precision=lax.Precision.HIGHEST)
    gam_imag = jnp.einsum("kg,gsv->ksv", one_hot, table_imag, precision=lax.Precision.HIGHEST)
    return (gam_real, gam_imag)


def color_apply(link_real, link_imag, spin_real, spin_imag, dagger):
    outs_real = []
    outs_imag = []
    for c in range(3):
        summed_real = 0.0
        summed_imag = 0.0
        for d in range(3):
            if dagger:
                coef_real = link_real[d, c]
                coef_imag = -link_imag[d, c]
            else:
                coef_real = link_real[c, d]
                coef_imag = link_imag[c, d]
            coef_real = coef_real[..., None, None, :, :]
            coef_imag = coef_imag[..., None, None, :, :]
            part_real = spin_real[..., d, :, :]
            part_imag = spin_imag[..., d, :, :]
            summed_real = summed_real + coef_real * part_real - coef_imag * part_imag
            summed_imag = summed_imag + coef_real * part_imag + coef_imag * part_real
        outs_real.append(summed_real)
        outs_imag.append(summed_imag)
    return (jnp.stack(outs_real, axis=-3), jnp.stack(outs_imag, axis=-3))


def spin_apply(matrix, spin_real, spin_imag):
    outs_real = []
    outs_imag = []
    for t in range(4):
        summed_real = 0.0
        summed_imag = 0.0
        for s in range(4):
            coef_real = float(matrix[0][t, s])
            coef_imag = float(matrix[1][t, s])
            if coef_real == 0.0 and coef_imag == 0.0:
                continue
            part_real = spin_real[..., s, :, :, :, :]
            part_imag = spin_imag[..., s, :, :, :, :]
            summed_real = summed_real + coef_real * part_real - coef_imag * part_imag
            summed_imag = summed_imag + coef_real * part_imag + coef_imag * part_real
        outs_real.append(summed_real)
        outs_imag.append(summed_imag)
    return (jnp.stack(outs_real, axis=-5), jnp.stack(outs_imag, axis=-5))


def plane_roll(spinor, offset, along_y, width_x):
    initial = spinor.shape
    gridded = spinor.reshape(initial[:-1] + (initial[-1] // width_x, width_x))
    gridded = jnp.roll(gridded, offset, axis=-2 if along_y else -1)
    return gridded.reshape(initial)


def current(fwd_real, fwd_imag, link_real, link_imag, up_z, down_z, width_x):
    singles, clifford = gamma_tables()
    summed_real = 0.0
    summed_imag = 0.0
    for direction in range(3):
        single_real, single_imag = singles[direction]
        minus_proj = ((np.eye(4) - single_real) / 2.0, -single_imag / 2.0)
        plus_proj = ((np.eye(4) + single_real) / 2.0, single_imag / 2.0)
        if direction < 2:
            along_y = direction == 1
            up_real = plane_roll(fwd_real, -1, along_y, width_x)
            up_imag = plane_roll(fwd_imag, -1, along_y, width_x)
            back_real, back_imag = color_apply(
                link_real[direction], link_imag[direction], fwd_real, fwd_imag, True
            )
            down_real = plane_roll(back_real, 1, along_y, width_x)
            down_imag = plane_roll(back_imag, 1, along_y, width_x)
        else:
            up_real, up_imag = up_z
            down_real, down_imag = down_z
        hop_real, hop_imag = color_apply(
            link_real[direction], link_imag[direction], up_real, up_imag, False
        )
        ahead_real, ahead_imag = spin_apply(minus_proj, hop_real, hop_imag)
        behind_real, behind_imag = spin_apply(plus_proj, down_real, down_imag)
        summed_real = summed_real + ahead_real - behind_real
        summed_imag = summed_imag + ahead_imag - behind_imag
    return (summed_real, summed_imag)


def phase_list(momenta, z_start, layers, plane_size, width_x, width_y, full_z):
    sites = jnp.arange(plane_size, dtype=jnp.int32)
    coord_x = sites % width_x
    coord_y = sites // width_x
    coord_z = z_start + jnp.arange(layers, dtype=jnp.int32)
    result = []
    for number in range(momenta.shape[0]):
        frac_plane = jnp.mod(momenta[number, 0] * coord_x, width_x).astype(jnp.float32) / float(
            width_x
        )
        frac_plane = frac_plane + jnp.mod(momenta[number, 1] * coord_y, width_y).astype(
            jnp.float32
        ) / float(width_y)
        frac_depth = jnp.mod(momenta[number, 2] * coord_z, full_z).astype(jnp.float32) / float(
            full_z
        )
        result.append(2.0 * math.pi * (frac_depth[:, None] + frac_plane[None, :]))
    return result


def contract(back_piece, weave_re, weave_im, thetas, gam_real, gam_imag, scaling):
    back_real = back_piece[0].astype(jnp.float32)
    back_imag = back_piece[1].astype(jnp.float32)
    slab_times, spins, columns = (back_real.shape[0], back_real.shape[1], back_real.shape[2])
    blocks = []
    for theta in thetas:
        cosine = jnp.cos(theta)
        sine_part = jnp.sin(theta)
        rot_real = (cosine * back_real - sine_part * back_imag).astype(jnp.bfloat16)
        rot_imag = (sine_part * back_real + cosine * back_imag).astype(jnp.bfloat16)
        stacked = jnp.concatenate(
            [
                rot_real.reshape(slab_times, spins, columns, -1),
                rot_imag.reshape(slab_times, spins, columns, -1),
            ],
            axis=-1,
        )
        pair_real = jnp.einsum(
            "usak,uvbk->usvab", stacked, weave_re, preferred_element_type=jnp.float32
        )
        pair_imag = jnp.einsum(
            "usak,uvbk->usvab", stacked, weave_im, preferred_element_type=jnp.float32
        )
        out_real = jnp.einsum(
            "ksv,usvab->kuab", gam_real, pair_real, precision=lax.Precision.HIGHEST
        ) - jnp.einsum("ksv,usvab->kuab", gam_imag, pair_imag, precision=lax.Precision.HIGHEST)
        out_imag = jnp.einsum(
            "ksv,usvab->kuab", gam_real, pair_imag, precision=lax.Precision.HIGHEST
        ) + jnp.einsum("ksv,usvab->kuab", gam_imag, pair_real, precision=lax.Precision.HIGHEST)
        blocks.append(jnp.stack([out_real, out_imag]) * scaling)
    return jnp.stack(blocks, axis=1)


def body(backward, forward, gauge_links, momenta, gamma_list):
    layers = forward.shape[5]
    plane_size = forward.shape[6]
    width_x = LX
    full_z = layers * lax.axis_size("space")
    z_start = lax.axis_index("space") * layers
    fwd_real = forward[0].astype(jnp.float32)
    fwd_imag = forward[1].astype(jnp.float32)
    link_real = gauge_links[0].astype(jnp.float32)
    link_imag = gauge_links[1].astype(jnp.float32)
    back_real, back_imag = color_apply(link_real[2], link_imag[2], fwd_real, fwd_imag, True)
    hopped = jnp.stack([back_real, back_imag])
    carried = passed_along(as_sent(hopped[:, :, :, :, :, -1:, :]), "space", 1)
    down_both = jnp.concatenate([carried, hopped[:, :, :, :, :, :-1, :]], axis=5)
    down_z = (down_both[0], down_both[1])
    following = passed_along(forward[:, :, :, :, :, :1, :], "space", -1)
    up_both = jnp.concatenate([forward[:, :, :, :, :, 1:, :], following], axis=5).astype(
        jnp.float32
    )
    up_z = (up_both[0], up_both[1])
    weave_real, weave_imag = current(
        fwd_real, fwd_imag, link_real, link_imag, up_z, down_z, width_x
    )
    slab_times = forward.shape[1]
    flat_real = weave_real.astype(jnp.bfloat16).reshape(slab_times, 4, forward.shape[3], -1)
    flat_imag = weave_imag.astype(jnp.bfloat16).reshape(slab_times, 4, forward.shape[3], -1)
    weave_re = jnp.concatenate([flat_real, flat_imag], axis=-1)
    weave_im = jnp.concatenate([flat_imag, -flat_real], axis=-1)
    thetas = phase_list(
        momenta, z_start, layers, plane_size, width_x, plane_size // width_x, full_z
    )
    gam_real, gam_imag = chosen_gammas(gamma_list)
    scaling = 1.0 / math.sqrt(3.0 * plane_size * full_z)
    partial_value = contract(
        gathered_copies(backward, "spin", 3),
        weave_re,
        weave_im,
        thetas,
        gam_real,
        gam_imag,
        scaling,
    )
    return summed_on_arrival(partial_value.astype(jnp.bfloat16), "space", 4)


def solution(mesh):
    in_specs = (
        P("parts", "tm", None, "spin", None, "space", None),
        P("parts", "tm", None, "spin", None, "space", None),
        P("parts", None, None, None, "tm", "space", None),
        P(),
        P(),
    )
    out_specs = P("parts", None, None, "tm", "space", "spin")
    return jax.shard_map(body, mesh=mesh, in_specs=in_specs, out_specs=out_specs, check_vma=False)
```

profile of v0, /device:TPU:40, one launch (start us, length us, event | category | flops | bytes accessed | tf_op | source)
XLA Modules:
  0.0 181.6 jit_solution(3506864021027311004)
XLA Ops:
  0.0 45.5 %collective-permute-start = (bf16[2,1,4,32,3,1,128]{6,3,4,2,5,1,0:T(8,128)(2,1)}, bf16[2,1,4,32,3,1,128]{6,3,4,2,5,1,0:T(8,128)(2,1)}, u32[]{:S(2)}, u32[]{:S(2)}) collective-permute-start(bf16[2,1,4,32,3,1,128]{6,3,4,2,5,1,0:T(8,128)(2,1)} %bitcast.738), channel_id=1, source_target_pairs={{0,248},{8,0},{16,8},{24,16},{32,24},{40,32},{48,40},{56,48},{64,5... | collective-permute-start | bytes 589832 | tf_op jit(solution)/shard_map/ppermute | solution.py:19
  45.5 0.9 fusion.43
  46.4 0.9 fusion.42
  47.3 0.8 slice_convert_fusion.5
  49.6 0.7 pad_maximum_fusion.14
  50.3 1.9 %collective-permute-start.1 = (bf16[2,1,4,32,3,1,128]{6,3,4,2,5,1,0:T(8,128)(2,1)}, bf16[2,1,4,32,3,1,128]{6,3,4,2,5,1,0:T(8,128)(2,1)}, u32[]{:S(2)}, u32[]{:S(2)}) collective-permute-start(bf16[2,1,4,32,3,1,128]{6,3,4,2,5,1,0:T(8,128)(2,1)} %pad_maximum_fusion.14), channel_id=1, source_target_pairs={{0,8},{8,16},{16,24},{24,32},{32,40},{40,48},{48,56},{56,64},{64,7... | collective-permute-start | bytes 589832 | tf_op jit(solution)/shard_map/ppermute | solution.py:19
  52.2 0.8 broadcast_in_dim.2
  53.0 4.2 %all-to-all-start = ((bf16[2,2,1,4,32,3,1,128]{7,4,6,5,3,2,1,0:T(8,128)(2,1)}), bf16[2,2,1,4,32,3,1,128]{7,4,6,5,3,2,1,0:T(8,128)(2,1)}, u32[]{:S(2)}, u32[]{:S(2)}) async-start(bf16[2,2,1,4,32,3,1,128]{7,4,6,5,3,2,1,0:T(8,128)(2,1)} %broadcast_in_dim.2), calls=%async_computation | async-start | bytes 786432 | tf_op jit(solution)/shard_map/all_to_all | solution.py:30
  61.6 0.7 add_subtract_fusion.5
  63.5 0.8 slice.941
  64.9 0.8 slice.936
  65.7 1.3 pad_maximum_fusion.5
  67.0 2.2 %reshape.3609 = f32[1,4,32,3,1,128]{5,2,3,1,4,0:T(8,128)} reshape(f32[1,4,32,3,1,4,32]{6,5,2,3,1,4,0:T(4,128)} %pad_maximum_fusion.5) | data formatting | bytes 393216 | tf_op jit(solution)/shard_map/reshape | solution.py:129
  69.2 1.4 pad_maximum_fusion.4
  71.0 1.0 multiply_subtract_fusion.8
  72.0 0.8 multiply_subtract_fusion.7
  72.9 0.7 add_subtract_fusion.7
  81.2 0.7 add_subtract_fusion.11
  91.5 1.3 fusion.75
  92.8 1.2 fusion.77
  94.1 1.4 fusion.79
  95.6 1.1 slice_convert_fusion.1
  97.9 1.2 subtract_convert_fusion.2
  99.3 1.0 convert_element_type.378
  100.6 1.0 convert_element_type.377
  104.1 1.3 convolution_bitcast_fusion.4
  110.2 0.8 convolution_bitcast_fusion.12
  114.2 1.3 convolution_bitcast_fusion.6
  116.5 1.6 fusion.5
  119.3 1.5 reshape.3662
  120.7 59.1 %all_to_all.10 = bf16[32,2,3072]{2,1,0:T(2,128)(2,1)S(1)} all-to-all(bf16[32,2,3072]{2,1,0:T(2,128)(2,1)S(1)} %reshape.3662), channel_id=1, replica_groups=mesh['parts'=2,'space'=32,'tm'=4,'spin'=2] {'space'}, dimensions={0} | all-to-all | bytes 786432 | tf_op jit(solution)/shard_map/all_to_all | solution.py:44
  179.9 0.7 reshape.3663
  (423 shorter events, 36.0 us)
Async XLA Ops:
  0.0 52.2 %copy-start.23 = (bf16[2,1,4,32,3,1,128]{6,3,5,4,2,1,0:T(8,128)(2,1)S(1)}, bf16[2,1,4,32,3,1,128]{6,3,5,4,2,1,0:T(8,128)(2,1)}, u32[]{:S(2)}) copy-start(bf16[2,1,4,32,3,1,128]{6,3,5,4,2,1,0:T(8,128)(2,1)} %param.7) | copy-start | bytes 589828
  0.0 100.6 %collective-permute-start = (bf16[2,1,4,32,3,1,128]{6,3,4,2,5,1,0:T(8,128)(2,1)}, bf16[2,1,4,32,3,1,128]{6,3,4,2,5,1,0:T(8,128)(2,1)}, u32[]{:S(2)}, u32[]{:S(2)}) collective-permute-start(bf16[2,1,4,32,3,1,128]{6,3,4,2,5,1,0:T(8,128)(2,1)} %bitcast.738), channel_id=1, source_target_pairs={{0,248},{8,0},{16,8},{24,16},{32,24},{40,32},{48,40},{56,48},{64,5... | collective-permute-start | bytes 589832 | tf_op jit(solution)/shard_map/ppermute | solution.py:19
  50.3 49.0 %collective-permute-start.1 = (bf16[2,1,4,32,3,1,128]{6,3,4,2,5,1,0:T(8,128)(2,1)}, bf16[2,1,4,32,3,1,128]{6,3,4,2,5,1,0:T(8,128)(2,1)}, u32[]{:S(2)}, u32[]{:S(2)}) collective-permute-start(bf16[2,1,4,32,3,1,128]{6,3,4,2,5,1,0:T(8,128)(2,1)} %pad_maximum_fusion.14), channel_id=1, source_target_pairs={{0,8},{8,16},{16,24},{24,32},{32,40},{40,48},{48,56},{56,64},{64,7... | collective-permute-start | bytes 589832 | tf_op jit(solution)/shard_map/ppermute | solution.py:19
  53.0 42.5 %all-to-all-start = ((bf16[2,2,1,4,32,3,1,128]{7,4,6,5,3,2,1,0:T(8,128)(2,1)}), bf16[2,2,1,4,32,3,1,128]{7,4,6,5,3,2,1,0:T(8,128)(2,1)}, u32[]{:S(2)}, u32[]{:S(2)}) async-start(bf16[2,2,1,4,32,3,1,128]{7,4,6,5,3,2,1,0:T(8,128)(2,1)} %broadcast_in_dim.2), calls=%async_computation | async-start | bytes 786432 | tf_op jit(solution)/shard_map/all_to_all | solution.py:30
  70.6 2.2 %copy-start.52 = (f32[128]{0:T(128)S(1)}, f32[128]{0:T(128)}, u32[]{:S(2)}) copy-start(f32[128]{0:T(128)} %copy-done.51) | copy-start | bytes 1540
  70.6 2.2 %copy-start.54 = (f32[128]{0:T(128)S(1)}, f32[128]{0:T(128)}, u32[]{:S(2)}) copy-start(f32[128]{0:T(128)} %copy-done.53) | copy-start | bytes 1540
  70.6 2.2 %copy-start.56 = (f32[128]{0:T(128)S(1)}, f32[128]{0:T(128)}, u32[]{:S(2)}) copy-start(f32[128]{0:T(128)} %copy-done.55) | copy-start | bytes 1540
  70.6 2.2 %copy-start.86 = (f32[128]{0:T(128)S(1)}, f32[128]{0:T(128)}, u32[]{:S(2)}) copy-start(f32[128]{0:T(128)} %get-tuple-element.151) | copy-start | bytes 1540
  70.6 2.2 %copy-start.87 = (f32[128]{0:T(128)S(1)}, f32[128]{0:T(128)}, u32[]{:S(2)}) copy-start(f32[128]{0:T(128)} %get-tuple-element.152) | copy-start | bytes 1540
  70.6 2.2 %copy-start.88 = (f32[128]{0:T(128)S(1)}, f32[128]{0:T(128)}, u32[]{:S(2)}) copy-start(f32[128]{0:T(128)} %get-tuple-element.153) | copy-start | bytes 1540
  75.0 2.7 %copy-start.62 = (f32[128]{0:T(128)}, f32[128]{0:T(128)S(1)}, u32[]{:S(2)}) copy-start(f32[128]{0:T(128)S(1)} %get-tuple-element.191) | copy-start | bytes 1540
  75.0 2.7 %copy-start.64 = (f32[128]{0:T(128)}, f32[128]{0:T(128)S(1)}, u32[]{:S(2)}) copy-start(f32[128]{0:T(128)S(1)} %get-tuple-element.192) | copy-start | bytes 1540
  75.0 2.7 %copy-start.66 = (f32[128]{0:T(128)}, f32[128]{0:T(128)S(1)}, u32[]{:S(2)}) copy-start(f32[128]{0:T(128)S(1)} %get-tuple-element.193) | copy-start | bytes 1540
  75.0 2.7 %copy-start.71 = (f32[128]{0:T(128)}, f32[128]{0:T(128)S(1)}, u32[]{:S(2)}) copy-start(f32[128]{0:T(128)S(1)} %get-tuple-element.187) | copy-start | bytes 1540
  75.0 2.7 %copy-start.73 = (f32[128]{0:T(128)}, f32[128]{0:T(128)S(1)}, u32[]{:S(2)}) copy-start(f32[128]{0:T(128)S(1)} %get-tuple-element.194) | copy-start | bytes 1540
  75.0 2.7 %copy-start.75 = (f32[128]{0:T(128)}, f32[128]{0:T(128)S(1)}, u32[]{:S(2)}) copy-start(f32[128]{0:T(128)S(1)} %get-tuple-element.195) | copy-start | bytes 1540
  85.7 3.3 %copy-start.9 = (f32[1,1,32,3,1,128]{5,2,3,1,4,0:T(8,128)S(1)}, f32[1,1,32,3,1,128]{5,2,3,1,4,0:T(8,128)}, u32[]{:S(2)}) copy-start(f32[1,1,32,3,1,128]{5,2,3,1,4,0:T(8,128)} %get-tuple-element.75) | copy-start | bytes 147460
  85.7 3.3 %copy-start.7 = (f32[1,1,32,3,1,128]{5,2,3,1,4,0:T(8,128)S(1)}, f32[1,1,32,3,1,128]{5,2,3,1,4,0:T(8,128)}, u32[]{:S(2)}) copy-start(f32[1,1,32,3,1,128]{5,2,3,1,4,0:T(8,128)} %get-tuple-element.78) | copy-start | bytes 147460
  85.8 3.3 %copy-start.25 = (f32[1,1,32,3,1,128]{5,2,3,1,4,0:T(8,128)S(1)}, f32[1,1,32,3,1,128]{5,2,3,1,4,0:T(8,128)}, u32[]{:S(2)}) copy-start(f32[1,1,32,3,1,128]{5,2,3,1,4,0:T(8,128)} %get-tuple-element.79) | copy-start | bytes 147460
  85.9 3.4 %copy-start.14 = (f32[1,1,32,3,1,128]{5,2,3,1,4,0:T(8,128)S(1)}, f32[1,1,32,3,1,128]{5,2,3,1,4,0:T(8,128)}, u32[]{:S(2)}) copy-start(f32[1,1,32,3,1,128]{5,2,3,1,4,0:T(8,128)} %get-tuple-element.69) | copy-start | bytes 147460
  85.9 3.4 %copy-start.12 = (f32[1,1,32,3,1,128]{5,2,3,1,4,0:T(8,128)S(1)}, f32[1,1,32,3,1,128]{5,2,3,1,4,0:T(8,128)}, u32[]{:S(2)}) copy-start(f32[1,1,32,3,1,128]{5,2,3,1,4,0:T(8,128)} %get-tuple-element.71) | copy-start | bytes 147460
  86.0 3.5 %copy-start.13 = (f32[1,1,32,3,1,128]{5,2,3,1,4,0:T(8,128)S(1)}, f32[1,1,32,3,1,128]{5,2,3,1,4,0:T(8,128)}, u32[]{:S(2)}) copy-start(f32[1,1,32,3,1,128]{5,2,3,1,4,0:T(8,128)} %get-tuple-element.73) | copy-start | bytes 147460
  86.0 3.5 %copy-start.22 = (f32[1,1,32,3,1,128]{5,2,3,1,4,0:T(8,128)S(1)}, f32[1,1,32,3,1,128]{5,2,3,1,4,0:T(8,128)}, u32[]{:S(2)}) copy-start(f32[1,1,32,3,1,128]{5,2,3,1,4,0:T(8,128)} %get-tuple-element.61) | copy-start | bytes 147460
  86.0 3.6 %copy-start.20 = (f32[1,1,32,3,1,128]{5,2,3,1,4,0:T(8,128)S(1)}, f32[1,1,32,3,1,128]{5,2,3,1,4,0:T(8,128)}, u32[]{:S(2)}) copy-start(f32[1,1,32,3,1,128]{5,2,3,1,4,0:T(8,128)} %get-tuple-element.64) | copy-start | bytes 147460
  86.0 3.7 %copy-start.21 = (f32[1,1,32,3,1,128]{5,2,3,1,4,0:T(8,128)S(1)}, f32[1,1,32,3,1,128]{5,2,3,1,4,0:T(8,128)}, u32[]{:S(2)}) copy-start(f32[1,1,32,3,1,128]{5,2,3,1,4,0:T(8,128)} %get-tuple-element.65) | copy-start | bytes 147460
  86.0 3.8 %copy-start.19 = (f32[1,1,32,3,1,128]{5,2,3,1,4,0:T(8,128)S(1)}, f32[1,1,32,3,1,128]{5,2,3,1,4,0:T(8,128)}, u32[]{:S(2)}) copy-start(f32[1,1,32,3,1,128]{5,2,3,1,4,0:T(8,128)} %get-tuple-element.66) | copy-start | bytes 147460
  97.4 1.6 copy-start.99
  100.4 1.4 copy-start.34
  103.4 1.9 %copy-start.30 = (bf16[1,4,64,384]{3,2,1,0:T(8,128)(2,1)S(1)}, bf16[1,4,64,384]{3,2,1,0:T(8,128)(2,1)}, u32[]{:S(2)}) copy-start(bf16[1,4,64,384]{3,2,1,0:T(8,128)(2,1)} %get-tuple-element.7) | copy-start | bytes 589828
  103.4 1.9 %copy-start.31 = (bf16[1,4,64,384]{3,2,1,0:T(8,128)(2,1)S(1)}, bf16[1,4,64,384]{3,2,1,0:T(8,128)(2,1)}, u32[]{:S(2)}) copy-start(bf16[1,4,64,384]{3,2,1,0:T(8,128)(2,1)} %get-tuple-element.8) | copy-start | bytes 589828
  103.5 2.2 %copy-start.27 = (bf16[1,4,64,384]{3,2,1,0:T(8,128)(2,1)S(1)}, bf16[1,4,64,384]{3,2,1,0:T(8,128)(2,1)}, u32[]{:S(2)}) copy-start(bf16[1,4,64,384]{3,2,1,0:T(8,128)(2,1)} %get-tuple-element.15) | copy-start | bytes 589828
  103.5 2.2 %copy-start.28 = (bf16[1,4,64,384]{3,2,1,0:T(8,128)(2,1)S(1)}, bf16[1,4,64,384]{3,2,1,0:T(8,128)(2,1)}, u32[]{:S(2)}) copy-start(bf16[1,4,64,384]{3,2,1,0:T(8,128)(2,1)} %get-tuple-element.16) | copy-start | bytes 589828
  (72 other events, 74.3 us)
where the time goes:
time: 183 us; the launch traced here: 182 us
  blocking collectives  59.1 us (32%)
  starting transfers between devices  51.6 us (28%)
  other arithmetic  29.5 us (16%)
  local copies, waits for them, and re-layouts  23.9 us (13%)
  matrix products  12.6 us (7%)
  between operations  5.02 us (3%)
    all_to_all x1, blocking collectives, summed_on_arrival(): lax.all_to_all(pieces, axis, split_axis=0, concat_axis=0, tiled=True)  59.1 us
    ppermute x2, starting transfers between devices, passed_along(): return lax.ppermute(value, axis, pairs)  47.4 us
    concatenate x8, other arithmetic, plane_roll(): gridded = jnp.roll(gridded, offset, axis=-2 if along_y else -1)  5.65 us
    reshape x8, local copies, waits for them, and re-layouts, plane_roll(): return gridded.reshape(initial)  4.68 us
    sub x12, other arithmetic, spin_apply(): summed_real = summed_real + coef_real * part_real - coef_imag * part_imag  4.43 us
    slice x10, local copies, waits for them, and re-layouts, plane_roll(): gridded = jnp.roll(gridded, offset, axis=-2 if along_y else -1)  4.34 us
    all_to_all x1, starting transfers between devices, copy_for_each(): return lax.all_to_all(copies, axis, split_axis=0, concat_axis=0, tiled=True)  4.2 us
    sub x12, other arithmetic, color_apply(): summed_real = summed_real + coef_real * part_real - coef_imag * part_imag  4.19 us
  transfers between devices with their start and end apart: 3, of which 0 were waited for; matrix products, arithmetic and copies ran while one was open for 24% of the time, Pallas kernels for 0%

commit v1 on v0

v1 whole, which is shorter than its diff:
```python
import functools
import math

import jax
import jax.numpy as jnp
import numpy as np
from jax import lax
from jax.experimental import pallas as pl
from jax.experimental.pallas import tpu as pltpu
from jax.sharding import PartitionSpec as P

MESH = pl.DeviceIdType.MESH
LX = 32
F32 = jnp.float32
BF16 = jnp.bfloat16

CENTERS = {-8: (-7, -9), -11: (-10, -12), -14: (-13, -15), 4: (3, 5), 7: (6, 8), 10: (9, 11), 13: (12, 14), 16: (15,)}
DIRECT = (-1, -2, -3, -4, -5, -6, 1, 2)
CENTER_ORDER = (4, 7, 10, 13, 16, -8, -11, -14)
CHILD = tuple((child, q) for q in CENTER_ORDER for child in CENTERS[q])
OFFSETS = DIRECT + tuple(c for c, _ in CHILD) + CENTER_ORDER
SLOT = {o: i for i, o in enumerate(OFFSETS)}


def gamma_tables():
    zeros = np.zeros((4, 4))
    gx = np.array([[0, 0, 0, 1j], [0, 0, 1j, 0], [0, -1j, 0, 0], [-1j, 0, 0, 0]])
    gy = np.array([[0, 0, 0, -1], [0, 0, 1, 0], [0, 1, 0, 0], [-1, 0, 0, 0]]) + 0j
    gz = np.array([[0, 0, 1j, 0], [0, 0, 0, -1j], [-1j, 0, 0, 0], [0, 1j, 0, 0]])
    gt = np.array([[0, 0, 1, 0], [0, 0, 0, 1], [1, 0, 0, 0], [0, 1, 0, 0]]) + 0j
    singles = [gx, gy, gz, gt]
    basis = []
    for number in range(16):
        mat = np.eye(4) + 0j
        for which in range(4):
            if number >> which & 1:
                mat = mat @ singles[which]
        basis.append(mat)
    return singles, np.stack(basis)


def contraction_table(nmom):
    _, basis = gamma_tables()
    table = np.zeros((2, 128, 256), np.float32)
    for g in range(16):
        for p in range(nmom):
            for a in range(2):
                row = g * 2 * nmom + p * 2 + a
                for s in range(4):
                    for s2 in range(4):
                        value = basis[g][s, s2]
                        for ri_out, ri_in, coef in ((0, 0, value.real), (0, 1, -value.imag), (1, 0, value.imag), (1, 1, value.real)):
                            table[ri_out, row, ((s2 * 2 + ri_in) * nmom + p) * 8 + s * 2 + a] = coef
    return table


def times_unit(coef, value):
    re, im = value
    if coef == 1:
        return re, im
    if coef == -1:
        return -re, -im
    if coef == 1j:
        return -im, re
    assert coef == -1j
    return im, -re


def plus(x, y):
    return x[0] + y[0], x[1] + y[1]


def projector(mu, sign):
    singles, _ = gamma_tables()
    mat = np.eye(4) + sign * singles[mu]
    result = []
    for s in range(2):
        t = [t for t in (2, 3) if mat[s, t] != 0][0]
        result.append((s, t, complex(mat[s, t]), complex(mat[t, s])))
    return result


def kernel(n, nmom, ngam, scaling,
           mom_ref, gam_ref, b_hbm, f_hbm, u_hbm, t_hbm, o_ref,
           fv, uv, tv, bb, ff, uf, bf, wv, lh, rh, rp, ck, hup_s, hup_r, hdn_s, hdn_r, cbuf, rbuf, cs, lmat,
           lsem, bsem, hsem, csend, crecv, ready, readyp):
    z = lax.axis_index("space")
    spin = lax.axis_index("spin")
    rows = fv.shape[3]

    load_f = pltpu.make_async_copy(f_hbm, fv, lsem.at[0])
    load_u = pltpu.make_async_copy(u_hbm, uv, lsem.at[1])
    load_b = pltpu.make_async_copy(b_hbm, bb.at[spin], lsem.at[2])
    load_t = pltpu.make_async_copy(t_hbm, tv, lsem.at[3])
    for copy in (load_f, load_u, load_b, load_t):
        copy.start()

    links = {1, n - 1} | {(-o) % n for o in DIRECT + CENTER_ORDER} | {o % n for o in DIRECT + CENTER_ORDER}
    links |= {(q - c) % n for c, q in CHILD} | {(c - q) % n for c, q in CHILD}
    peers = sorted(links)
    at = {d: i for i, d in enumerate(peers)}

    def chip(d):
        return {"space": lax.rem(z + d, n)}

    barrier = pltpu.get_barrier_semaphore()
    count = jnp.where(spin == 0, 1, 0)
    for d in peers:
        count = count + jnp.where(z + d >= n, 1, 0)

        @pl.when(z + d < n)
        def _():
            pl.semaphore_signal(barrier, inc=1, device_id=chip(d), device_id_type=MESH)

    @pl.when(spin == 1)
    def _():
        pl.semaphore_signal(barrier, inc=1, device_id={"spin": 0}, device_id_type=MESH)

    @pl.when(count > 0)
    def _():
        pl.semaphore_wait(barrier, count)

    for d in peers:
        @pl.when(z + d >= n)
        def _():
            pl.semaphore_signal(ready.at[at[n - d]], inc=1, device_id=chip(d), device_id_type=MESH)

    @pl.when(spin == 0)
    def _():
        pl.semaphore_signal(readyp, inc=1, device_id={"spin": 1}, device_id_type=MESH)

    seen = set()

    def reach(d):
        if d not in seen:
            seen.add(d)

            @pl.when(z + d < n)
            def _():
                pl.semaphore_wait(ready.at[at[d]], 1)

    load_f.wait()
    load_u.wait()
    ff[...] = fv[...].astype(F32)
    for i in range(uv.shape[0]):
        uf[i] = uv[i].astype(F32)

    def link(mu, c, d, dagger):
        if dagger:
            return uf[mu * 9 + d * 3 + c, 0:1, :], -uf[mu * 9 + d * 3 + c, 1:2, :]
        return uf[mu * 9 + c * 3 + d, 0:1, :], uf[mu * 9 + c * 3 + d, 1:2, :]

    def colored(mu, dagger, h):
        out = []
        for c in range(3):
            re = im = None
            for d in range(3):
                cr, ci = link(mu, c, d, dagger)
                hr, hi = h[d]
                pr, pi = cr * hr - ci * hi, cr * hi + ci * hr
                re, im = (pr, pi) if re is None else (re + pr, im + pi)
            out.append((re, im))
        return out

    def half(mu, sign, which, sl):
        s, t, alpha, beta = projector(mu, sign)[which]
        h = []
        for c in range(3):
            x = (ff[0, s, c, sl, :], ff[1, s, c, sl, :])
            y = (ff[0, t, c, sl, :], ff[1, t, c, sl, :])
            h.append(plus(x, times_unit(alpha, y)))
        return s, t, beta, h

    blocks = [pl.ds(i, 16) for i in range(0, rows, 16)]
    for which in range(2):
        for sl in blocks:
            _, _, _, h = half(2, -1, which, sl)
            for c in range(3):
                hup_s[0, which, c, sl, :] = h[c][0].astype(BF16)
                hup_s[1, which, c, sl, :] = h[c][1].astype(BF16)
    send_up = pltpu.make_async_remote_copy(hup_s, hup_r, hsem.at[0], hsem.at[1], device_id=chip(n - 1), device_id_type=MESH)
    for which in range(2):
        for sl in blocks:
            _, _, _, h = half(2, 1, which, sl)
            h = colored(2, True, h)
            for c in range(3):
                hdn_s[0, which, c, sl, :] = h[c][0].astype(BF16)
                hdn_s[1, which, c, sl, :] = h[c][1].astype(BF16)
    send_dn = pltpu.make_async_remote_copy(hdn_s, hdn_r, hsem.at[2], hsem.at[3], device_id=chip(1), device_id_type=MESH)

    @pl.when(z > 0)
    def _():
        send_up.start()

    @pl.when(z == n - 1)
    def _():
        send_dn.start()

    load_b.wait()

    @pl.when(spin == 1)
    def _():
        pl.semaphore_wait(readyp, 1)

    swap_b = pltpu.make_async_remote_copy(bb.at[spin], bb.at[spin], bsem.at[0], bsem.at[1], device_id={"spin": 1 - spin}, device_id_type=MESH)
    swap_b.start()

    @pl.when(z < n - 1)
    def _():
        pl.semaphore_wait(ready.at[at[1]], 1)
        send_dn.start()
    seen.add(1)

    sub = lax.broadcasted_iota(jnp.int32, (8, 128), 0)
    lane = lax.broadcasted_iota(jnp.int32, (8, 128), 1)
    x1, x2 = lane & (LX - 1), lane // LX
    width_y = 128 // LX

    def momentum(axis):
        value = jnp.full((8, 128), mom_ref[0, axis], jnp.int32)
        for p in range(1, nmom):
            value = jnp.where(sub == p, mom_ref[p, axis], value)
        return value

    turn = (((momentum(0) * x1) & (LX - 1)).astype(F32) / float(LX)
            + ((momentum(1) * x2) & (width_y - 1)).astype(F32) / float(width_y))
    turn = ((momentum(2) * z) & (n - 1)).astype(F32) / float(n) + turn
    theta = 2.0 * math.pi * turn
    cs[0] = jnp.cos(theta)
    cs[1] = jnp.sin(theta)

    first = lane[0:1, :] & (LX - 1)
    for mu in range(2):
        for which in range(2):
            for sl in blocks:
                for sign in (-1, 1):
                    s, t, beta, h = half(mu, sign, which, sl)
                    if sign == 1:
                        h = colored(mu, True, h)
                    moved = []
                    for pair in h:
                        if mu == 1:
                            moved.append(tuple(pltpu.roll(v, 128 - LX if sign == -1 else LX, 1) for v in pair))
                        elif sign == -1:
                            moved.append(tuple(jnp.where(first == LX - 1, pltpu.roll(v, LX - 1, 1), pltpu.roll(v, 127, 1)) for v in pair))
                        else:
                            moved.append(tuple(jnp.where(first == 0, pltpu.roll(v, 128 - (LX - 1), 1), pltpu.roll(v, 1, 1)) for v in pair))
                    h = moved
                    if sign == -1:
                        h = colored(mu, False, h)
                    for c in range(3):
                        other = times_unit(beta, h[c])
                        for ri in range(2):
                            if mu == 0 and sign == -1:
                                wv[ri, s, c, sl, :] = h[c][ri]
                                wv[ri, t, c, sl, :] = other[ri]
                            elif sign == -1:
                                wv[ri, s, c, sl, :] += h[c][ri]
                                wv[ri, t, c, sl, :] += other[ri]
                            else:
                                wv[ri, s, c, sl, :] -= h[c][ri]
                                wv[ri, t, c, sl, :] -= other[ri]

    load_t.wait()
    half_rows = nmom * ngam * 2
    r = lax.broadcasted_iota(jnp.int32, (half_rows, 128), 0)
    l2 = lax.broadcasted_iota(jnp.int32, (half_rows, 128), 1)
    k_of = (r >> 1) & (ngam - 1)
    p_of = r // (2 * ngam)
    g_of = jnp.full((half_rows, 128), gam_ref[0], jnp.int32)
    for k in range(1, ngam):
        g_of = jnp.where(k_of == k, gam_ref[k], g_of)
    hot = jnp.where(l2 == g_of * (2 * nmom) + p_of * 2 + (r & 1), 1.0, 0.0).astype(BF16)
    for ri in range(2):
        lmat[pl.ds(ri * half_rows, half_rows), :] = jnp.dot(hot, tv[ri], preferred_element_type=F32).astype(BF16)

    swap_b.wait_recv()
    bf[...] = bb[...].astype(F32)
    for s in range(4):
        for which in range(2):
            for c in range(3):
                for a in range(2):
                    br = bf.at[which, 0, s, c][pl.ds(a, 16, stride=2), :]
                    bi = bf.at[which, 1, s, c][pl.ds(a, 16, stride=2), :]
                    for p in range(nmom):
                        co, si = cs[0, p:p + 1, :], cs[1, p:p + 1, :]
                        at_row = pl.ds((p * 4 + s) * 64 + a * 32 + which * 16, 16)
                        lh[at_row, pl.ds(c * 128, 128)] = (co * br - si * bi).astype(BF16)
                        lh[at_row, pl.ds((3 + c) * 128, 128)] = (si * br + co * bi).astype(BF16)

    @pl.when(z == 0)
    def _():
        pl.semaphore_wait(ready.at[at[n - 1]], 1)
        send_up.start()
    seen.add(n - 1)

    send_up.wait_recv()
    for which in range(2):
        s, t, alpha, beta = projector(2, -1)[which]
        for sl in blocks:
            h = [(hup_r[0, which, c, sl, :].astype(F32), hup_r[1, which, c, sl, :].astype(F32)) for c in range(3)]
            h = colored(2, False, h)
            for c in range(3):
                other = times_unit(beta, h[c])
                for ri in range(2):
                    wv[ri, s, c, sl, :] += h[c][ri]
                    wv[ri, t, c, sl, :] += other[ri]
    send_dn.wait_recv()
    for which in range(2):
        s, t, alpha, beta = projector(2, 1)[which]
        for sl in blocks:
            start = sl.start
            for c in range(3):
                h = (hdn_r[0, which, c, sl, :].astype(F32), hdn_r[1, which, c, sl, :].astype(F32))
                other = times_unit(beta, h)
                for comp, value in ((s, h), (t, other)):
                    re = ((wv[0, comp, c, sl, :] - value[0]) * 0.5).astype(BF16)
                    im = ((wv[1, comp, c, sl, :] - value[1]) * 0.5).astype(BF16)
                    top, low = pl.ds(comp * rows + start, 16), pl.ds(4 * rows + comp * rows + start, 16)
                    rh[top, pl.ds(c * 128, 128)] = re
                    rh[top, pl.ds((3 + c) * 128, 128)] = im
                    rh[low, pl.ds(c * 128, 128)] = im
                    rh[low, pl.ds((3 + c) * 128, 128)] = -re

    for p in range(nmom):
        prod = lax.dot_general(lh[pl.ds(p * 256, 256), :], rh[...], (((1,), (1,)), ((), ())), preferred_element_type=F32)
        for j in range(8):
            for ri in range(2):
                rp[ri, pl.ds((p * 8 + j) * 40, 32), :] = prod[j * 32:(j + 1) * 32, ri * 128:(ri + 1) * 128]

    def partial(c):
        return [rp.at[ri][pl.ds(c, nmom * 8, stride=40), :] for ri in range(2)]

    def owner(o):
        return lax.rem(z + (-o) % n, n)

    copies = []

    def send(o, source, target):
        d = (target - o) % n
        reach(d)
        copy = pltpu.make_async_remote_copy(source, rbuf.at[SLOT[o]], csend.at[SLOT[o]], crecv.at[SLOT[o]], device_id=chip(d), device_id_type=MESH)
        copy.start()
        copies.append(copy)

    def arrived(o):
        pltpu.make_async_remote_copy(ck.at[0], rbuf.at[SLOT[o]], csend.at[SLOT[o]], crecv.at[SLOT[o]], device_id=chip(0), device_id_type=MESH).wait_recv()

    plain = [o for o in OFFSETS if o not in CENTERS]
    for i, o in enumerate(plain):
        ck[i] = jnp.concatenate(partial(owner(o)), axis=0).astype(BF16)
    for i, o in enumerate(plain):
        send(o, ck.at[i], dict(CHILD).get(o, 0))
    for i, q in enumerate(CENTER_ORDER):
        total = jnp.concatenate(partial(owner(q)), axis=0)
        for child in CENTERS[q]:
            arrived(child)
            total = total + rbuf[SLOT[child]].astype(F32)
        cbuf[i] = total.astype(BF16)
        send(q, cbuf.at[i], 0)

    total = jnp.concatenate(partial(z), axis=0)
    for o in DIRECT[6:] + CENTER_ORDER[:5] + CENTER_ORDER[:4:-1] + DIRECT[5::-1]:
        arrived(o)
        total = total + rbuf[SLOT[o]].astype(F32)
    stack = jnp.concatenate([total if s2 == 0 else pltpu.roll(total, 128 - s2 * rows, 1) for s2 in range(4)], axis=0)
    high = stack.astype(BF16)
    low = (stack - high.astype(F32)).astype(BF16)
    mat = lmat[:, 0:stack.shape[0]]
    out = jnp.dot(mat, high, preferred_element_type=F32) + jnp.dot(mat, low, preferred_element_type=F32)
    o_ref[...] = out[:, 0:rows] * scaling
    for d in peers:
        reach(d)
    for copy in copies:
        copy.wait_send()
    send_up.wait_send()
    send_dn.wait_send()
    swap_b.wait_send()


def solution(mesh):
    n = mesh.shape["space"]

    def body(backward, forward, gauge_links, momenta, gamma_list):
        cols, plane = forward.shape[3], forward.shape[6]
        nmom, ngam = momenta.shape[0], gamma_list.shape[0]
        scaling = 1.0 / math.sqrt(3.0 * plane * n)
        b = backward.transpose(0, 1, 2, 4, 5, 3, 6).reshape(2, 4, 3, cols, plane)
        f = forward.transpose(0, 1, 2, 4, 5, 3, 6).reshape(2, 4, 3, cols, plane)
        u = gauge_links.transpose(1, 2, 3, 4, 5, 0, 6).reshape(27, 2, plane)
        table = jnp.asarray(contraction_table(nmom), BF16)
        half_shape = (2, 2, 3, cols, plane)
        chunk = (nmom * 16, plane)
        n_rows = nmom * 4 * 2 * cols
        any_spec = pl.BlockSpec(memory_space=pl.ANY)
        smem = pl.BlockSpec(memory_space=pltpu.SMEM)
        n_links = len({1, n - 1} | {o % n for o in DIRECT + CENTER_ORDER} | {(-o) % n for o in DIRECT + CENTER_ORDER})
        out = pl.pallas_call(
            functools.partial(kernel, n, nmom, ngam, scaling),
            out_shape=jax.ShapeDtypeStruct((2 * nmom * ngam * 2, cols), F32),
            in_specs=[smem, smem, any_spec, any_spec, any_spec, any_spec],
            out_specs=pl.BlockSpec(memory_space=pltpu.VMEM),
            name="insertion",
            scratch_shapes=[
                pltpu.VMEM(f.shape, BF16),
                pltpu.VMEM(u.shape, BF16),
                pltpu.VMEM(table.shape, BF16),
                pltpu.VMEM((2, *b.shape), BF16),
                pltpu.VMEM(f.shape, F32),
                pltpu.VMEM(u.shape, F32),
                pltpu.VMEM((2, *b.shape), F32),
                pltpu.VMEM(f.shape, F32),
                pltpu.VMEM((n_rows, 6 * plane), BF16),
                pltpu.VMEM((8 * cols, 6 * plane), BF16),
                pltpu.VMEM((2, nmom * 8 * 40, plane), F32),
                pltpu.VMEM((len(OFFSETS) - len(CENTERS), *chunk), BF16),
                pltpu.VMEM(half_shape, BF16),
                pltpu.VMEM(half_shape, BF16),
                pltpu.VMEM(half_shape, BF16),
                pltpu.VMEM(half_shape, BF16),
                pltpu.VMEM((len(CENTERS), *chunk), BF16),
                pltpu.VMEM((len(OFFSETS), *chunk), BF16),
                pltpu.VMEM((2, 8, plane), F32),
                pltpu.VMEM((2 * nmom * ngam * 2, 256), BF16),
                pltpu.SemaphoreType.DMA((4,)),
                pltpu.SemaphoreType.DMA((2,)),
                pltpu.SemaphoreType.DMA((4,)),
                pltpu.SemaphoreType.DMA((len(OFFSETS),)),
                pltpu.SemaphoreType.DMA((len(OFFSETS),)),
                pltpu.SemaphoreType.REGULAR((n_links,)),
                pltpu.SemaphoreType.REGULAR,
            ],
            compiler_params=pltpu.CompilerParams(collective_id=0, has_side_effects=True, vmem_limit_bytes=67043328),
        )(momenta, gamma_list, b, f, u, table)
        return out.reshape(2, nmom, ngam, 1, 2, cols)

    in_specs = (
        P("parts", "tm", None, "spin", None, "space", None),
        P("parts", "tm", None, "spin", None, "space", None),
        P("parts", None, None, None, "tm", "space", None),
        P(),
        P(),
    )
    out_specs = P("parts", None, None, "tm", "space", "spin")
    return jax.shard_map(body, mesh=mesh, in_specs=in_specs, out_specs=out_specs, check_vma=False)
```

time: 183 us -> 88.2 us (0.48)
  the two profiles are of different devices: /device:TPU:40 before, /device:TPU:96 now
where the time goes in v1:
time: 88.2 us; the launch traced here: 88 us
  Pallas kernels  86.5 us (98%)
  local copies, waits for them, and re-layouts  1.54 us (2%)
    pallas_call x1, Pallas kernels, body(): pl.pallas_call(functools.partial(kernel, n, nmom, ngam, scaling), out_sha...  86.5 us

profile of v1, /device:TPU:96, one launch (start us, length us, event | category | flops | bytes accessed | tf_op | source)
XLA Modules:
  0.0 88.0 jit_solution(14816259439924700314)
XLA Ops:
  0.0 86.5 %insertion.1 = f32[192,32]{1,0:T(8,128)} custom-call(s32[3,3]{1,0:T(4,128)} %mom_ref.1, s32[16]{0:T(128)} %gam_ref.1, bf16[2,4,3,32,128]{4,3,2,1,0:T(8,128)(2,1)} %bitcast.17, bf16[2,4,3,32,128]{4,3,2,1,0:T(8,128)(2,1)} %bitcast.18, bf16[27,2,128]{2,1,0:T(2,128)(2,1)} %bitcast.19, bf16[2,128,256]{2,1,0:T(8,128)(2,1)} %constant.2.clone.t_hbm), custom_call_target="tpu_custom_call" | custom-call | tf_op jit(solution)/shard_map/insertion/pallas_call | solution.py:398
  86.5 1.5 %copy.11 = f32[2,3,16,1,2,32]{5,4,3,2,1,0:T(2,128)} copy(f32[2,3,16,1,2,32]{5,4,3,2,1,0:T(2,128)} %bitcast.16) | data formatting | bytes 49152

commit v2 on v1

--- a/solution.py
+++ b/solution.py
@@ -14,12 +14,7 @@
 F32 = jnp.float32
 BF16 = jnp.bfloat16
 
-CENTERS = {-8: (-7, -9), -11: (-10, -12), -14: (-13, -15), 4: (3, 5), 7: (6, 8), 10: (9, 11), 13: (12, 14), 16: (15,)}
-DIRECT = (-1, -2, -3, -4, -5, -6, 1, 2)
-CENTER_ORDER = (4, 7, 10, 13, 16, -8, -11, -14)
-CHILD = tuple((child, q) for q in CENTER_ORDER for child in CENTERS[q])
-OFFSETS = DIRECT + tuple(c for c, _ in CHILD) + CENTER_ORDER
-SLOT = {o: i for i, o in enumerate(OFFSETS)}
+STEP = 3
 
 
 def gamma_tables():
@@ -81,9 +76,9 @@
 
 
 def kernel(n, nmom, ngam, scaling,
-           mom_ref, gam_ref, b_hbm, f_hbm, u_hbm, t_hbm, o_ref,
-           fv, uv, tv, bb, ff, uf, bf, wv, lh, rh, rp, ck, hup_s, hup_r, hdn_s, hdn_r, cbuf, rbuf, cs, lmat,
-           lsem, bsem, hsem, csend, crecv, ready, readyp):
+           mom_hbm, gam_hbm, b_hbm, f_hbm, u_hbm, t_hbm, o_ref,
+           fv, uv, tv, bb, ff, uf, bf, wv, lh, rh, rp, hup_s, hup_r, hdn_s, hdn_r, c1, c2, crole, r1, r2, r3, cs, lmat, mom_ref, gam_ref,
+           lsem, bsem, hsem, csend, crecv, inside_sem, readyp):
     z = lax.axis_index("space")
     spin = lax.axis_index("spin")
     rows = fv.shape[3]
@@ -92,52 +87,53 @@
     load_u = pltpu.make_async_copy(u_hbm, uv, lsem.at[1])
     load_b = pltpu.make_async_copy(b_hbm, bb.at[spin], lsem.at[2])
     load_t = pltpu.make_async_copy(t_hbm, tv, lsem.at[3])
-    for copy in (load_f, load_u, load_b, load_t):
+    load_m = pltpu.make_async_copy(mom_hbm, mom_ref, lsem.at[4])
+    load_g = pltpu.make_async_copy(gam_hbm, gam_ref, lsem.at[5])
+    for copy in (load_f, load_u, load_b, load_t, load_m, load_g):
         copy.start()
-
-    links = {1, n - 1} | {(-o) % n for o in DIRECT + CENTER_ORDER} | {o % n for o in DIRECT + CENTER_ORDER}
-    links |= {(q - c) % n for c, q in CHILD} | {(c - q) % n for c, q in CHILD}
-    peers = sorted(links)
-    at = {d: i for i, d in enumerate(peers)}
 
     def chip(d):
         return {"space": lax.rem(z + d, n)}
 
+    def tell(sem, d):
+        pl.semaphore_signal(sem, inc=1, device_id=chip(d), device_id_type=MESH)
+
+    up, down = 0, 1
+    last = z == n - 1
+    near_in, two_in, three_in = inside_sem.at[0], inside_sem.at[1], inside_sem.at[2]
     barrier = pltpu.get_barrier_semaphore()
-    count = jnp.where(spin == 0, 1, 0)
-    for d in peers:
-        count = count + jnp.where(z + d >= n, 1, 0)
-
-        @pl.when(z + d < n)
-        def _():
-            pl.semaphore_signal(barrier, inc=1, device_id=chip(d), device_id_type=MESH)
+    up_later = jnp.logical_and(z > 0, jnp.logical_not(last))
+    down_later = z < 2
+
+    @pl.when(up_later)
+    def _():
+        tell(barrier, 1)
+
+    @pl.when(down_later)
+    def _():
+        tell(barrier, n - 1)
 
     @pl.when(spin == 1)
     def _():
         pl.semaphore_signal(barrier, inc=1, device_id={"spin": 0}, device_id_type=MESH)
 
+    count = jnp.where(up_later, 0, 1) + jnp.where(down_later, 0, 1) + jnp.where(spin == 0, 1, 0)
+
     @pl.when(count > 0)
     def _():
         pl.semaphore_wait(barrier, count)
 
-    for d in peers:
-        @pl.when(z + d >= n)
-        def _():
-            pl.semaphore_signal(ready.at[at[n - d]], inc=1, device_id=chip(d), device_id_type=MESH)
+    @pl.when(jnp.logical_not(down_later))
+    def _():
+        tell(near_in.at[up], n - 1)
+
+    @pl.when(jnp.logical_not(up_later))
+    def _():
+        tell(near_in.at[down], 1)
 
     @pl.when(spin == 0)
     def _():
         pl.semaphore_signal(readyp, inc=1, device_id={"spin": 1}, device_id_type=MESH)
-
-    seen = set()
-
-    def reach(d):
-        if d not in seen:
-            seen.add(d)
-
-            @pl.when(z + d < n)
-            def _():
-                pl.semaphore_wait(ready.at[at[d]], 1)
 
     load_f.wait()
     load_u.wait()
@@ -188,14 +184,23 @@
                 hdn_s[1, which, c, sl, :] = h[c][1].astype(BF16)
     send_dn = pltpu.make_async_remote_copy(hdn_s, hdn_r, hsem.at[2], hsem.at[3], device_id=chip(1), device_id_type=MESH)
 
-    @pl.when(z > 0)
+    @pl.when(jnp.logical_not(down_later))
     def _():
         send_up.start()
 
-    @pl.when(z == n - 1)
-    def _():
-        send_dn.start()
-
+    @pl.when(up_later)
+    def _():
+        pl.semaphore_wait(near_in.at[up], 1)
+
+    send_dn.start()
+
+    @pl.when(down_later)
+    def _():
+        pl.semaphore_wait(near_in.at[down], 1)
+        send_up.start()
+
+    tell(two_in.at[up], n - 1)
+    tell(two_in.at[down], 1)
     load_b.wait()
 
     @pl.when(spin == 1)
@@ -204,13 +209,7 @@
 
     swap_b = pltpu.make_async_remote_copy(bb.at[spin], bb.at[spin], bsem.at[0], bsem.at[1], device_id={"spin": 1 - spin}, device_id_type=MESH)
     swap_b.start()
-
-    @pl.when(z < n - 1)
-    def _():
-        pl.semaphore_wait(ready.at[at[1]], 1)
-        send_dn.start()
-    seen.add(1)
-
+    load_m.wait()
     sub = lax.broadcasted_iota(jnp.int32, (8, 128), 0)
     lane = lax.broadcasted_iota(jnp.int32, (8, 128), 1)
     x1, x2 = lane & (LX - 1), lane // LX
@@ -262,6 +261,7 @@
                                 wv[ri, t, c, sl, :] -= other[ri]
 
     load_t.wait()
+    load_g.wait()
     half_rows = nmom * ngam * 2
     r = lax.broadcasted_iota(jnp.int32, (half_rows, 128), 0)
     l2 = lax.broadcasted_iota(jnp.int32, (half_rows, 128), 1)
@@ -287,12 +287,6 @@
                         at_row = pl.ds((p * 4 + s) * 64 + a * 32 + which * 16, 16)
                         lh[at_row, pl.ds(c * 128, 128)] = (co * br - si * bi).astype(BF16)
                         lh[at_row, pl.ds((3 + c) * 128, 128)] = (si * br + co * bi).astype(BF16)
-
-    @pl.when(z == 0)
-    def _():
-        pl.semaphore_wait(ready.at[at[n - 1]], 1)
-        send_up.start()
-    seen.add(n - 1)
 
     send_up.wait_recv()
     for which in range(2):
@@ -331,48 +325,95 @@
     def partial(c):
         return [rp.at[ri][pl.ds(c, nmom * 8, stride=40), :] for ri in range(2)]
 
-    def owner(o):
-        return lax.rem(z + (-o) % n, n)
-
-    copies = []
-
-    def send(o, source, target):
-        d = (target - o) % n
-        reach(d)
-        copy = pltpu.make_async_remote_copy(source, rbuf.at[SLOT[o]], csend.at[SLOT[o]], crecv.at[SLOT[o]], device_id=chip(d), device_id_type=MESH)
-        copy.start()
-        copies.append(copy)
-
-    def arrived(o):
-        pltpu.make_async_remote_copy(ck.at[0], rbuf.at[SLOT[o]], csend.at[SLOT[o]], crecv.at[SLOT[o]], device_id=chip(0), device_id_type=MESH).wait_recv()
-
-    plain = [o for o in OFFSETS if o not in CENTERS]
-    for i, o in enumerate(plain):
-        ck[i] = jnp.concatenate(partial(owner(o)), axis=0).astype(BF16)
-    for i, o in enumerate(plain):
-        send(o, ck.at[i], dict(CHILD).get(o, 0))
-    for i, q in enumerate(CENTER_ORDER):
-        total = jnp.concatenate(partial(owner(q)), axis=0)
-        for child in CENTERS[q]:
-            arrived(child)
-            total = total + rbuf[SLOT[child]].astype(F32)
-        cbuf[i] = total.astype(BF16)
-        send(q, cbuf.at[i], 0)
-
+    centers = crole.shape[1]
+    def part(side, m):
+        forward_owner = lax.rem(z + jnp.where(side == 0, m, n - m), n)
+        return jnp.concatenate(partial(forward_owner), axis=0)
+
+    def post(side, steps, source, target, which):
+        peer = {"space": lax.rem(z + jnp.where(side == 0, steps, n - steps), n)}
+        return pltpu.make_async_remote_copy(source, target, csend.at[side, which], crecv.at[side, which], device_id=peer, device_id_type=MESH)
+
+    def direct(side):
+        return post(side, 1, c1.at[side, pl.ds(centers, 1)], r1.at[side, pl.ds(centers, 1)], 0)
+
+    def near(side, i):
+        return post(side, 1, c1.at[side, pl.ds(i, 1)], r1.at[side, pl.ds(i, 1)], 1 + i)
+
+    def far(side, i):
+        return post(side, 2, c2.at[side, pl.ds(i, 1)], r2.at[side, pl.ds(i, 1)], 1 + centers + i)
+
+    def passed(side, i):
+        to = centers - 1 if i == 0 else i - 1
+        return post(side, 2 if i == 0 else STEP, crole.at[side, pl.ds(i, 1)], r3.at[side, pl.ds(to, 1)], 1 + 2 * centers + i)
+
+    def has_far(side, i):
+        m = STEP * i + 4
+        return m < n // 2 or (m == n // 2 and side == up)
+
+    levels = range(centers - 1, -1, -1)
+
+    def center(side, i):
+        total = part(side, STEP * i + 2)
+        near(side, i).wait_recv()
+        total = total + r1[side, i].astype(F32)
+        if has_far(side, i):
+            far(side, i).wait_recv()
+            total = total + r2[side, i].astype(F32)
+        if i < centers - 1:
+            passed(side, i + 1).wait_recv()
+            total = total + r3[side, i].astype(F32)
+        crole[side, i] = total.astype(BF16)
+        if i == centers - 1:
+            pl.semaphore_wait(three_in.at[side], 1)
+        passed(side, i).start()
+
+    for side in range(2):
+        c1[side, centers] = part(side, 1).astype(BF16)
+        for i in levels:
+            c1[side, i] = part(side, STEP * i + 3).astype(BF16)
+            if has_far(side, i):
+                c2[side, i] = part(side, STEP * i + 4).astype(BF16)
+    for side in range(2):
+        direct(side).start()
+    for side in range(2):
+        pl.semaphore_wait(two_in.at[side], 1)
+        tell(three_in.at[side], n - 1 if side == up else 1)
+        for i in levels:
+            if has_far(side, i):
+                far(side, i).start()
+            near(side, i).start()
+    def inside(i):
+        return z >= STEP * (centers - 1 - i) + 7
+
+    for i in levels:
+        @pl.when(inside(i))
+        def _():
+            center(0, i)
+    for i in levels:
+        center(1, i)
+    for i in levels:
+        @pl.when(jnp.logical_not(inside(i)))
+        def _():
+            center(0, i)
     total = jnp.concatenate(partial(z), axis=0)
-    for o in DIRECT[6:] + CENTER_ORDER[:5] + CENTER_ORDER[:4:-1] + DIRECT[5::-1]:
-        arrived(o)
-        total = total + rbuf[SLOT[o]].astype(F32)
+    for side in range(2):
+        direct(side).wait_recv()
+        passed(side, 0).wait_recv()
+        total = total + r1[side, centers].astype(F32) + r3[side, centers - 1].astype(F32)
     stack = jnp.concatenate([total if s2 == 0 else pltpu.roll(total, 128 - s2 * rows, 1) for s2 in range(4)], axis=0)
     high = stack.astype(BF16)
     low = (stack - high.astype(F32)).astype(BF16)
     mat = lmat[:, 0:stack.shape[0]]
     out = jnp.dot(mat, high, preferred_element_type=F32) + jnp.dot(mat, low, preferred_element_type=F32)
     o_ref[...] = out[:, 0:rows] * scaling
-    for d in peers:
-        reach(d)
-    for copy in copies:
-        copy.wait_send()
+    for side in range(2):
+        direct(side).wait_send()
+        for i in levels:
+            near(side, i).wait_send()
+            if has_far(side, i):
+                far(side, i).wait_send()
+            passed(side, i).wait_send()
     send_up.wait_send()
     send_dn.wait_send()
     swap_b.wait_send()
@@ -393,12 +434,11 @@
         chunk = (nmom * 16, plane)
         n_rows = nmom * 4 * 2 * cols
         any_spec = pl.BlockSpec(memory_space=pl.ANY)
-        smem = pl.BlockSpec(memory_space=pltpu.SMEM)
-        n_links = len({1, n - 1} | {o % n for o in DIRECT + CENTER_ORDER} | {(-o) % n for o in DIRECT + CENTER_ORDER})
+        centers = (n // 2 - 2) // STEP + 1
         out = pl.pallas_call(
             functools.partial(kernel, n, nmom, ngam, scaling),
             out_shape=jax.ShapeDtypeStruct((2 * nmom * ngam * 2, cols), F32),
-            in_specs=[smem, smem, any_spec, any_spec, any_spec, any_spec],
+            in_specs=[any_spec, any_spec, any_spec, any_spec, any_spec, any_spec],
             out_specs=pl.BlockSpec(memory_space=pltpu.VMEM),
             name="insertion",
             scratch_shapes=[
@@ -413,21 +453,26 @@
                 pltpu.VMEM((n_rows, 6 * plane), BF16),
                 pltpu.VMEM((8 * cols, 6 * plane), BF16),
                 pltpu.VMEM((2, nmom * 8 * 40, plane), F32),
-                pltpu.VMEM((len(OFFSETS) - len(CENTERS), *chunk), BF16),
                 pltpu.VMEM(half_shape, BF16),
                 pltpu.VMEM(half_shape, BF16),
                 pltpu.VMEM(half_shape, BF16),
                 pltpu.VMEM(half_shape, BF16),
-                pltpu.VMEM((len(CENTERS), *chunk), BF16),
-                pltpu.VMEM((len(OFFSETS), *chunk), BF16),
+                pltpu.VMEM((2, centers + 1, *chunk), BF16),
+                pltpu.VMEM((2, centers, *chunk), BF16),
+                pltpu.VMEM((2, centers, *chunk), BF16),
+                pltpu.VMEM((2, centers + 1, *chunk), BF16),
+                pltpu.VMEM((2, centers, *chunk), BF16),
+                pltpu.VMEM((2, centers, *chunk), BF16),
                 pltpu.VMEM((2, 8, plane), F32),
                 pltpu.VMEM((2 * nmom * ngam * 2, 256), BF16),
-                pltpu.SemaphoreType.DMA((4,)),
+                pltpu.SMEM(momenta.shape, jnp.int32),
+                pltpu.SMEM(gamma_list.shape, jnp.int32),
+                pltpu.SemaphoreType.DMA((6,)),
                 pltpu.SemaphoreType.DMA((2,)),
                 pltpu.SemaphoreType.DMA((4,)),
-                pltpu.SemaphoreType.DMA((len(OFFSETS),)),
-                pltpu.SemaphoreType.DMA((len(OFFSETS),)),
-                pltpu.SemaphoreType.REGULAR((n_links,)),
+                pltpu.SemaphoreType.DMA((2, 1 + 3 * centers)),
+                pltpu.SemaphoreType.DMA((2, 1 + 3 * centers)),
+                pltpu.SemaphoreType.REGULAR((3, 2)),
                 pltpu.SemaphoreType.REGULAR,
             ],
             compiler_params=pltpu.CompilerParams(collective_id=0, has_side_effects=True, vmem_limit_bytes=67043328),

time: 88.2 us -> 67.9 us (0.77)
  the two profiles are of different devices: /device:TPU:96 before, /device:TPU:40 now
where the time goes in v2:
time: 67.9 us; the launch traced here: 67.7 us
  Pallas kernels  66.2 us (97%)
  local copies, waits for them, and re-layouts  1.54 us (2%)
    pallas_call x1, Pallas kernels, body(): pl.pallas_call(functools.partial(kernel, n, nmom, ngam, scaling), out_sha...  66.2 us
    unnamed x1, local copies, waits for them, and re-layouts  1.54 us

profile of v2, /device:TPU:40, one launch (start us, length us, event | category | flops | bytes accessed | tf_op | source)
XLA Modules:
  0.0 67.7 jit_solution(12713251075766709305)
XLA Ops:
  0.0 66.2 %insertion.1 = f32[192,32]{1,0:T(8,128)} custom-call(s32[3,3]{1,0:T(4,128)} %mom_hbm.1, s32[16]{0:T(128)} %gam_hbm.1, bf16[2,4,3,32,128]{4,3,2,1,0:T(8,128)(2,1)} %bitcast.17, bf16[2,4,3,32,128]{4,3,2,1,0:T(8,128)(2,1)} %bitcast.18, bf16[27,2,128]{2,1,0:T(2,128)(2,1)} %bitcast.19, bf16[2,128,256]{2,1,0:T(8,128)(2,1)} %constant.2.clone.t_hbm), custom_call_target="tpu_custom_call" | custom-call | tf_op jit(solution)/shard_map/insertion/pallas_call | solution.py:438
  66.2 1.5 %copy.11 = f32[2,3,16,1,2,32]{5,4,3,2,1,0:T(2,128)} copy(f32[2,3,16,1,2,32]{5,4,3,2,1,0:T(2,128)} %bitcast.16) | data formatting | bytes 49152

commit v3 on v2

--- a/solution.py
+++ b/solution.py
@@ -15,6 +15,7 @@
 BF16 = jnp.bfloat16
 
 STEP = 3
+REACH = STEP + 2
 
 
 def gamma_tables():
@@ -100,8 +101,13 @@
 
     up, down = 0, 1
     last = z == n - 1
-    near_in, two_in, three_in = inside_sem.at[0], inside_sem.at[1], inside_sem.at[2]
+    near_in, two_in = inside_sem.at[0], inside_sem.at[1]
     barrier = pltpu.get_barrier_semaphore()
+    def hear(side, distance):
+        pl.semaphore_wait(inside_sem.at[distance - 1, side], 1)
+        if distance < REACH:
+            tell(inside_sem.at[distance, side], n - 1 if side == up else 1)
+
     up_later = jnp.logical_and(z > 0, jnp.logical_not(last))
     down_later = z < 2
 
@@ -288,6 +294,11 @@
                         lh[at_row, pl.ds(c * 128, 128)] = (co * br - si * bi).astype(BF16)
                         lh[at_row, pl.ds((3 + c) * 128, 128)] = (si * br + co * bi).astype(BF16)
 
+    for distance in range(2, REACH + 1):
+        @pl.when(z > distance)
+        def _():
+            hear(down, distance)
+    hear(up, 2)
     send_up.wait_recv()
     for which in range(2):
         s, t, alpha, beta = projector(2, -1)[which]
@@ -344,8 +355,9 @@
         return post(side, 2, c2.at[side, pl.ds(i, 1)], r2.at[side, pl.ds(i, 1)], 1 + centers + i)
 
     def passed(side, i):
-        to = centers - 1 if i == 0 else i - 1
-        return post(side, 2 if i == 0 else STEP, crole.at[side, pl.ds(i, 1)], r3.at[side, pl.ds(to, 1)], 1 + 2 * centers + i)
+        to = (0, centers - 1)[i] if i < 2 else i - 1
+        steps = STEP * i + 2 if i < 2 else STEP
+        return post(side, steps, crole.at[side, pl.ds(i, 1)], r3.at[side, pl.ds(to, 1)], 1 + 2 * centers + i)
 
     def has_far(side, i):
         m = STEP * i + 4
@@ -360,12 +372,10 @@
         if has_far(side, i):
             far(side, i).wait_recv()
             total = total + r2[side, i].astype(F32)
-        if i < centers - 1:
+        if 0 < i < centers - 1:
             passed(side, i + 1).wait_recv()
             total = total + r3[side, i].astype(F32)
         crole[side, i] = total.astype(BF16)
-        if i == centers - 1:
-            pl.semaphore_wait(three_in.at[side], 1)
         passed(side, i).start()
 
     for side in range(2):
@@ -374,33 +384,54 @@
             c1[side, i] = part(side, STEP * i + 3).astype(BF16)
             if has_far(side, i):
                 c2[side, i] = part(side, STEP * i + 4).astype(BF16)
+    def hear_late(distance):
+        @pl.when(z <= distance)
+        def _():
+            hear(down, distance)
+
     for side in range(2):
         direct(side).start()
     for side in range(2):
-        pl.semaphore_wait(two_in.at[side], 1)
-        tell(three_in.at[side], n - 1 if side == up else 1)
+        if side == down:
+            hear_late(2)
         for i in levels:
             if has_far(side, i):
                 far(side, i).start()
             near(side, i).start()
+    hear(up, 3)
     def inside(i):
-        return z >= STEP * (centers - 1 - i) + 7
-
-    for i in levels:
+        return z >= STEP * (centers - 1 - i if i else 0) + 7
+
+    order = [i for i in levels if i > 1] + [0]
+
+    def inner(i):
         @pl.when(inside(i))
         def _():
-            center(0, i)
-    for i in levels:
-        center(1, i)
-    for i in levels:
+            center(up, i)
+
+    for i in order:
+        inner(i)
+        if i == centers - 1:
+            hear(up, 4)
+    hear(up, REACH)
+    inner(1)
+    center(down, 0)
+    hear_late(3)
+    for i in order[:-1]:
+        center(down, i)
+    for distance in range(4, REACH + 1):
+        hear_late(distance)
+    center(down, 1)
+    for i in [*order, 1]:
         @pl.when(jnp.logical_not(inside(i)))
         def _():
-            center(0, i)
+            center(up, i)
     total = jnp.concatenate(partial(z), axis=0)
     for side in range(2):
         direct(side).wait_recv()
         passed(side, 0).wait_recv()
-        total = total + r1[side, centers].astype(F32) + r3[side, centers - 1].astype(F32)
+        passed(side, 1).wait_recv()
+        total = total + r1[side, centers].astype(F32) + r3[side, 0].astype(F32) + r3[side, centers - 1].astype(F32)
     stack = jnp.concatenate([total if s2 == 0 else pltpu.roll(total, 128 - s2 * rows, 1) for s2 in range(4)], axis=0)
     high = stack.astype(BF16)
     low = (stack - high.astype(F32)).astype(BF16)
@@ -433,7 +464,7 @@
         half_shape = (2, 2, 3, cols, plane)
         chunk = (nmom * 16, plane)
         n_rows = nmom * 4 * 2 * cols
-        any_spec = pl.BlockSpec(memory_space=pl.ANY)
+        any_spec = pl.BlockSpec(memory_space=pltpu.MemorySpace.HBM)
         centers = (n // 2 - 2) // STEP + 1
         out = pl.pallas_call(
             functools.partial(kernel, n, nmom, ngam, scaling),
@@ -472,11 +503,11 @@
                 pltpu.SemaphoreType.DMA((4,)),
                 pltpu.SemaphoreType.DMA((2, 1 + 3 * centers)),
                 pltpu.SemaphoreType.DMA((2, 1 + 3 * centers)),
-                pltpu.SemaphoreType.REGULAR((3, 2)),
+                pltpu.SemaphoreType.REGULAR((REACH, 2)),
                 pltpu.SemaphoreType.REGULAR,
             ],
-            compiler_params=pltpu.CompilerParams(collective_id=0, has_side_effects=True, vmem_limit_bytes=67043328),
-        )(momenta, gamma_list, b, f, u, table)
+            compiler_params=pltpu.CompilerParams(collective_id=0, has_side_effects=True, vmem_limit_bytes=40 * 2**20),
+        )(*[pltpu.with_memory_space_constraint(v, pltpu.MemorySpace.HBM) for v in (momenta, gamma_list, b, f, u, table)])
         return out.reshape(2, nmom, ngam, 1, 2, cols)
 
     in_specs = (

time: 67.9 us -> 63.5 us (0.935)
  Pallas kernels: 66.2 us -> 62.7 us
  local copies, waits for them, and re-layouts: 1.54 us -> 0.64 us
    pallas_call x1, Pallas kernels: 66.2 us -> 62.7 us  [body(): pl.pallas_call(functools.partial(kernel, n, nmom, ngam, scaling), out_sha...]
    unnamed x1, local copies, waits for them, and re-layouts: 1.54 us -> 0.64 us
where the time goes in v3:
time: 63.5 us; the launch traced here: 63.3 us
  Pallas kernels  62.7 us (99%)
  local copies, waits for them, and re-layouts  0.64 us (1%)
    pallas_call x1, Pallas kernels, body(): pl.pallas_call(functools.partial(kernel, n, nmom, ngam, scaling), out_sha...  62.7 us

profile of v3, /device:TPU:40, one launch (start us, length us, event | category | flops | bytes accessed | tf_op | source)
XLA Modules:
  0.0 63.3 jit_solution(3156684341668555410)
XLA Ops:
  0.0 62.7 %insertion.1 = f32[192,32]{1,0:T(8,128)S(1)} custom-call(s32[3,3]{1,0:T(4,128)} %mom_hbm.1, s32[16]{0:T(128)} %gam_hbm.1, bf16[2,4,3,32,128]{4,3,2,1,0:T(8,128)(2,1)} %bitcast.17, bf16[2,4,3,32,128]{4,3,2,1,0:T(8,128)(2,1)} %bitcast.18, bf16[27,2,128]{2,1,0:T(2,128)(2,1)} %bitcast.19, bf16[2,128,256]{2,1,0:T(8,128)(2,1)} %constant.2.clone.t_hbm), custom_call_target="tpu_custom_call" | custom-call | tf_op jit(solution)/shard_map/insertion/pallas_call | solution.py:469
  62.7 0.6 %copy.11 = f32[2,3,16,1,2,32]{5,4,3,2,1,0:T(2,128)} copy(f32[2,3,16,1,2,32]{5,4,3,2,1,0:T(2,128)S(1)} %bitcast.16) | data formatting | bytes 49152

commit v4 on v3

--- a/solution.py
+++ b/solution.py
@@ -327,11 +327,10 @@
                     rh[low, pl.ds(c * 128, 128)] = im
                     rh[low, pl.ds((3 + c) * 128, 128)] = -re
 
-    for p in range(nmom):
-        prod = lax.dot_general(lh[pl.ds(p * 256, 256), :], rh[...], (((1,), (1,)), ((), ())), preferred_element_type=F32)
-        for j in range(8):
-            for ri in range(2):
-                rp[ri, pl.ds((p * 8 + j) * 40, 32), :] = prod[j * 32:(j + 1) * 32, ri * 128:(ri + 1) * 128]
+    prod = lax.dot_general(lh[...], rh[...], (((1,), (1,)), ((), ())), preferred_element_type=F32)
+    for j in range(nmom * 8):
+        for ri in range(2):
+            rp[ri, pl.ds(j * 40, 32), :] = prod[j * 32:(j + 1) * 32, ri * 128:(ri + 1) * 128]
 
     def partial(c):
         return [rp.at[ri][pl.ds(c, nmom * 8, stride=40), :] for ri in range(2)]
@@ -361,7 +360,7 @@
 
     def has_far(side, i):
         m = STEP * i + 4
-        return m < n // 2 or (m == n // 2 and side == up)
+        return m < n // 2 or (m == n // 2 and side == down)
 
     levels = range(centers - 1, -1, -1)
 
@@ -402,7 +401,7 @@
     def inside(i):
         return z >= STEP * (centers - 1 - i if i else 0) + 7
 
-    order = [i for i in levels if i > 1] + [0]
+    order = [i for i in levels if i > 2] + [0, 2]
 
     def inner(i):
         @pl.when(inside(i))
@@ -417,8 +416,9 @@
     inner(1)
     center(down, 0)
     hear_late(3)
-    for i in order[:-1]:
-        center(down, i)
+    for i in levels:
+        if i > 1:
+            center(down, i)
     for distance in range(4, REACH + 1):
         hear_late(distance)
     center(down, 1)

time: 63.5 us -> 63 us (level)
  no operation moved by 1% of the time
where the time goes in v4:
time: 63 us; the launch traced here: 62.8 us
  Pallas kernels  62.2 us (99%)
  local copies, waits for them, and re-layouts  0.64 us (1%)
    pallas_call x1, Pallas kernels, body(): pl.pallas_call(functools.partial(kernel, n, nmom, ngam, scaling), out_sha...  62.2 us

profile of v4, /device:TPU:40, one launch (start us, length us, event | category | flops | bytes accessed | tf_op | source)
XLA Modules:
  0.0 62.8 jit_solution(808632582908834487)
XLA Ops:
  0.0 62.2 %insertion.1 = f32[192,32]{1,0:T(8,128)S(1)} custom-call(s32[3,3]{1,0:T(4,128)} %mom_hbm.1, s32[16]{0:T(128)} %gam_hbm.1, bf16[2,4,3,32,128]{4,3,2,1,0:T(8,128)(2,1)} %bitcast.17, bf16[2,4,3,32,128]{4,3,2,1,0:T(8,128)(2,1)} %bitcast.18, bf16[27,2,128]{2,1,0:T(2,128)(2,1)} %bitcast.19, bf16[2,128,256]{2,1,0:T(8,128)(2,1)} %constant.2.clone.t_hbm), custom_call_target="tpu_custom_call" | custom-call | tf_op jit(solution)/shard_map/insertion/pallas_call | solution.py:469
  62.2 0.6 %copy.11 = f32[2,3,16,1,2,32]{5,4,3,2,1,0:T(2,128)} copy(f32[2,3,16,1,2,32]{5,4,3,2,1,0:T(2,128)S(1)} %bitcast.16) | data formatting | bytes 49152

commit v5 on v4

--- a/solution.py
+++ b/solution.py
@@ -85,7 +85,7 @@
     rows = fv.shape[3]
 
     load_f = pltpu.make_async_copy(f_hbm, fv, lsem.at[0])
-    load_u = pltpu.make_async_copy(u_hbm, uv, lsem.at[1])
+    load_u = pltpu.make_async_copy(u_hbm, uv.at[pl.ds(0, u_hbm.shape[0])], lsem.at[1])
     load_b = pltpu.make_async_copy(b_hbm, bb.at[spin], lsem.at[2])
     load_t = pltpu.make_async_copy(t_hbm, tv, lsem.at[3])
     load_m = pltpu.make_async_copy(mom_hbm, mom_ref, lsem.at[4])
@@ -144,7 +144,7 @@
     load_f.wait()
     load_u.wait()
     ff[...] = fv[...].astype(F32)
-    for i in range(uv.shape[0]):
+    for i in range(u_hbm.shape[0]):
         uf[i] = uv[i].astype(F32)
 
     def link(mu, c, d, dagger):
@@ -281,7 +281,7 @@
         lmat[pl.ds(ri * half_rows, half_rows), :] = jnp.dot(hot, tv[ri], preferred_element_type=F32).astype(BF16)
 
     swap_b.wait_recv()
-    bf[...] = bb[...].astype(F32)
+    bf[0:2] = bb[...].astype(F32)
     for s in range(4):
         for which in range(2):
             for c in range(3):
@@ -474,16 +474,16 @@
             name="insertion",
             scratch_shapes=[
                 pltpu.VMEM(f.shape, BF16),
-                pltpu.VMEM(u.shape, BF16),
+                pltpu.VMEM((u.shape[0] + 9, *u.shape[1:]), BF16),
                 pltpu.VMEM(table.shape, BF16),
                 pltpu.VMEM((2, *b.shape), BF16),
                 pltpu.VMEM(f.shape, F32),
-                pltpu.VMEM(u.shape, F32),
-                pltpu.VMEM((2, *b.shape), F32),
+                pltpu.VMEM((u.shape[0] + 9, *u.shape[1:]), F32),
+                pltpu.VMEM((3, *b.shape), F32),
                 pltpu.VMEM(f.shape, F32),
                 pltpu.VMEM((n_rows, 6 * plane), BF16),
                 pltpu.VMEM((8 * cols, 6 * plane), BF16),
-                pltpu.VMEM((2, nmom * 8 * 40, plane), F32),
+                pltpu.VMEM((2, nmom * 8 * 40 + 40, plane), F32),
                 pltpu.VMEM(half_shape, BF16),
                 pltpu.VMEM(half_shape, BF16),
                 pltpu.VMEM(half_shape, BF16),
@@ -494,7 +494,7 @@
                 pltpu.VMEM((2, centers + 1, *chunk), BF16),
                 pltpu.VMEM((2, centers, *chunk), BF16),
                 pltpu.VMEM((2, centers, *chunk), BF16),
-                pltpu.VMEM((2, 8, plane), F32),
+                pltpu.VMEM((3, 8, plane), F32),
                 pltpu.VMEM((2 * nmom * ngam * 2, 256), BF16),
                 pltpu.SMEM(momenta.shape, jnp.int32),
                 pltpu.SMEM(gamma_list.shape, jnp.int32),

time: 63 us -> 63 us (level)
  no operation moved by 1% of the time
where the time goes in v5:
time: 63 us; the launch traced here: 62.8 us
  Pallas kernels  62.2 us (99%)
  local copies, waits for them, and re-layouts  0.64 us (1%)
    pallas_call x1, Pallas kernels, body(): pl.pallas_call(functools.partial(kernel, n, nmom, ngam, scaling), out_sha...  62.2 us

profile of v5, /device:TPU:40, one launch (start us, length us, event | category | flops | bytes accessed | tf_op | source)
XLA Modules:
  0.0 62.8 jit_solution(7846833107443762320)
XLA Ops:
  0.0 62.2 %insertion.1 = f32[192,32]{1,0:T(8,128)S(1)} custom-call(s32[3,3]{1,0:T(4,128)} %mom_hbm.1, s32[16]{0:T(128)} %gam_hbm.1, bf16[2,4,3,32,128]{4,3,2,1,0:T(8,128)(2,1)} %bitcast.17, bf16[2,4,3,32,128]{4,3,2,1,0:T(8,128)(2,1)} %bitcast.18, bf16[27,2,128]{2,1,0:T(2,128)(2,1)} %bitcast.19, bf16[2,128,256]{2,1,0:T(8,128)(2,1)} %constant.2.clone.t_hbm), custom_call_target="tpu_custom_call" | custom-call | tf_op jit(solution)/shard_map/insertion/pallas_call | solution.py:469
  62.2 0.6 %copy.11 = f32[2,3,16,1,2,32]{5,4,3,2,1,0:T(2,128)} copy(f32[2,3,16,1,2,32]{5,4,3,2,1,0:T(2,128)S(1)} %bitcast.16) | data formatting | bytes 49152
